TPU v7x, 32 devices: a whole 2x2x4 slice. The times are simulated.
32 devices in a mesh: tm: 2 (over x), chan: 4 (over y, core), bl: 4 (over z).
Axes of the slice: x: 2, y: 2, z: 4, core: 2. Of those that a mesh axis runs over, the one named last changes fastest.
Arguments:
- voltages: bfloat16 [2, 256, 128, 512], P(None, ('chan', 'bl'), None, 'tm'), may hold values from -6 to 6
Outputs:
- visibilities: bfloat16 [2, 128, 4, 256, 256], P(None, ('chan', 'bl'), 'tm')
All inputs are finite; a program needn't handle non-finite values.
Results may differ from a plain program's by a relative error of at most 0.0051.
Values may be sent and summed in bfloat16 or wider, within the bound.
A program may use at most 64 MiB of HBM per device.

v0:
```python
import jax
import jax.numpy as jnp
from jax import lax
from jax.sharding import PartitionSpec as P

HALF = 128


def passed_along(block, axis, distance):
    devices = range(lax.axis_size(axis))
    route = [(i - distance, i) for i in devices if i - distance in devices]
    return lax.ppermute(block, axis, route)


def tapers(length):
    steps = jnp.arange(length, dtype=jnp.float32)
    taper_early = jnp.sin(jnp.pi * (steps + 0.5) / (2.0 * length))
    taper_late = jnp.sin(jnp.pi * (steps + 0.5 + length) / (2.0 * length))
    return (taper_early, taper_late)


def weighted(block, taper):
    return (block.astype(jnp.float32) * taper).astype(jnp.bfloat16)


def products(stacked):
    signals = stacked.shape[0] // 2
    gram = jnp.einsum("pct,qct->cpq", stacked, stacked, preferred_element_type=jnp.float32)
    real_part = gram[:, :signals, :signals] + gram[:, signals:, signals:]
    imag_part = gram[:, signals:, :signals] - gram[:, :signals, signals:]
    return (real_part, imag_part)


def local(voltages):
    turned = lax.all_to_all(voltages, ("chan", "bl"), split_axis=2, concat_axis=1, tiled=True)
    signals = turned.shape[1]
    channels = turned.shape[2]
    samples = turned.shape[3]
    halves = samples // HALF
    scale = 1.0 / HALF
    taper_early, taper_late = tapers(HALF)
    stacked = turned.reshape(2 * signals, channels, samples)
    lates = []
    earlies = []
    for index in range(halves):
        piece = stacked[:, :, index * HALF : (index + 1) * HALF]
        lates.append(products(weighted(piece, taper_late)))
        if index + 1 < halves:
            earlies.append(products(weighted(piece, taper_early)))
    tail = turned[:, :, :, samples - HALF :]
    received = passed_along(tail, "tm", 1)
    previous = products(weighted(received.reshape(2 * signals, channels, HALF), taper_early))
    real_list = []
    imag_list = []
    for index in range(halves):
        late_real, late_imag = lates[index]
        real_list.append(((late_real + previous[0]) * scale).astype(jnp.bfloat16))
        imag_list.append(((late_imag + previous[1]) * scale).astype(jnp.bfloat16))
        if index + 1 < halves:
            previous = earlies[index]
    return jnp.stack([jnp.stack(real_list, 1), jnp.stack(imag_list, 1)], 0)


def solution(mesh):
    return jax.shard_map(
        local,
        mesh=mesh,
        in_specs=(P(None, ("chan", "bl"), None, "tm"),),
        out_specs=P(None, ("chan", "bl"), "tm", None, None),
        check_vma=False,
    )
```

profile of v0, /device:TPU:0, one launch (start us, length us, event | category | flops | bytes accessed | tf_op | source)
XLA Modules:
  0.0 100.2 jit_solution(14008793336782749242)
XLA Ops:
  0.0 2.8 %copy.22 = bf16[2,16,128,256]{3,1,0,2:T(8,128)(2,1)S(1)} copy(bf16[2,16,128,256]{3,2,1,0:T(8,128)(2,1)} %param.1) | data formatting | bytes 4194304 | tf_op args[0]
  2.8 56.5 %all_to_all.18 = bf16[2,16,128,256]{3,1,0,2:T(8,128)(2,1)S(1)} all-to-all(bf16[2,16,128,256]{3,1,0,2:T(8,128)(2,1)S(1)} %copy.22), channel_id=1, replica_groups=mesh['tm'=2,'chan'=4,'bl'=4] {'chan','bl'}, dimensions={2} | all-to-all | bytes 4194304 | tf_op jit(solution)/shard_map/all_to_all | solution.py:35
  59.3 1.7 %copy.24 = bf16[2,16,16,8,256]{4,3,2,1,0:T(8,128)(2,1)S(1)} copy(bf16[2,16,16,8,256]{4,2,0,3,1:T(8,128)(2,1)S(1)} %bitcast.24) | data formatting | bytes 4194304 | tf_op jit(solution)/shard_map/all_to_all | solution.py:35
  61.0 0.1 slice.79
  61.1 3.6 %collective-permute-start = (bf16[2,256,8,128]{3,2,1,0:T(8,128)(2,1)S(1)}, bf16[2,256,8,128]{3,2,1,0:T(8,128)(2,1)S(1)}, u32[]{:S(2)}, u32[]{:S(2)}) collective-permute-start(bf16[2,256,8,128]{3,2,1,0:T(8,128)(2,1)S(1)} %slice.79), channel_id=1, source_target_pairs={{0,16},{1,17},{2,18},{3,19},{4,20},{5,21},{6,22},{7,23},{8,24},{9,... | collective-permute-start | bytes 3145736 | tf_op jit(solution)/shard_map/ppermute | solution.py:12
  64.7 0.1 multiply_sine_fusion
  64.8 22.0 %collective-permute-done = bf16[2,256,8,128]{3,2,1,0:T(8,128)(2,1)S(1)} collective-permute-done((bf16[2,256,8,128]{3,2,1,0:T(8,128)(2,1)S(1)}, bf16[2,256,8,128]{3,2,1,0:T(8,128)(2,1)S(1)}, u32[]{:S(2)}, u32[]{:S(2)}) %collective-permute-start) | collective-permute-done | bytes 1048608 | tf_op jit(solution)/shard_map/ppermute | solution.py:12
  86.8 0.8 fusion
  87.7 1.3 %fusion.23 = f32[8,512,512]{2,1,0:T(8,128)S(1)} fusion(bf16[512,8,128]{2,1,0:T(8,128)(2,1)S(1)} %get-tuple-element.12), kind=kOutput, calls=%fused_computation.38 | convolution fusion | flops 536870912 | bytes 9437184 | tf_op jit(solution)/shard_map/pct,qct->cpq/dot_general | solution.py:28
  88.9 1.3 %fusion.25 = f32[8,512,512]{2,1,0:T(8,128)S(1)} fusion(bf16[512,8,128]{2,1,0:T(8,128)(2,1)S(1)} %get-tuple-element.9), kind=kOutput, calls=%fused_computation.40 | convolution fusion | flops 536870912 | bytes 9437184 | tf_op jit(solution)/shard_map/pct,qct->cpq/dot_general | solution.py:28
  90.2 1.3 %fusion.19 = f32[8,512,512]{2,1,0:T(8,128)S(1)} fusion(bf16[512,8,128]{2,1,0:T(8,128)(2,1)S(1)} %get-tuple-element.11), kind=kOutput, calls=%fused_computation.34 | convolution fusion | flops 536870912 | bytes 9437184 | tf_op jit(solution)/shard_map/pct,qct->cpq/dot_general | solution.py:28
  91.5 1.3 %fusion.21 = f32[8,512,512]{2,1,0:T(8,128)S(1)} fusion(bf16[512,8,128]{2,1,0:T(8,128)(2,1)S(1)} %get-tuple-element.10), kind=kOutput, calls=%fused_computation.36 | convolution fusion | flops 536870912 | bytes 9437184 | tf_op jit(solution)/shard_map/pct,qct->cpq/dot_general | solution.py:28
  92.7 2.2 %fusion.15 = (bf16[8,1,256,256]{3,2,0,1:T(8,128)(2,1)S(1)}, bf16[8,1,256,256]{3,2,0,1:T(8,128)(2,1)S(1)}) fusion(f32[8,512,512]{2,1,0:T(8,128)S(1)} %fusion.23, f32[8,512,512]{2,1,0:T(8,128)S(1)} %fusion.25), kind=kLoop, calls=%fused_computation.30 | loop fusion | flops 5242880 | bytes 18874368 | tf_op jit(solution)/shard_map/stack | solution.py:61
  94.9 2.2 %fusion.16 = (bf16[8,1,256,256]{3,2,0,1:T(8,128)(2,1)S(1)}, bf16[8,1,256,256]{3,2,0,1:T(8,128)(2,1)S(1)}) fusion(f32[8,512,512]{2,1,0:T(8,128)S(1)} %fusion.19, f32[8,512,512]{2,1,0:T(8,128)S(1)} %fusion.21), kind=kLoop, calls=%fused_computation.31 | loop fusion | flops 5242880 | bytes 18874368 | tf_op jit(solution)/shard_map/stack | solution.py:61
  97.2 0.2 maximum_bitcast_fusion
  97.4 0.2 maximum_bitcast_fusion.1
  97.6 0.4 pad_maximum_fusion
  98.0 2.3 %copy.34 = bf16[2,8,2,256,256]{4,3,2,1,0:T(8,128)(2,1)} copy(bf16[2,8,2,256,256]{4,3,1,2,0:T(8,128)(2,1)S(1)} %pad_maximum_fusion) | data formatting | bytes 8388608 | tf_op jit(solution)/shard_map/stack | solution.py:61
Async XLA Ops:
  61.1 25.8 %collective-permute-start = (bf16[2,256,8,128]{3,2,1,0:T(8,128)(2,1)S(1)}, bf16[2,256,8,128]{3,2,1,0:T(8,128)(2,1)S(1)}, u32[]{:S(2)}, u32[]{:S(2)}) collective-permute-start(bf16[2,256,8,128]{3,2,1,0:T(8,128)(2,1)S(1)} %slice.79), channel_id=1, source_target_pairs={{0,16},{1,17},{2,18},{3,19},{4,20},{5,21},{6,22},{7,23},{8,24},{9,... | collective-permute-start | bytes 3145736 | tf_op jit(solution)/shard_map/ppermute | solution.py:12
where the time goes:
time: 100 us
  blocking collectives  56.5 us (56%)
  waiting for transfers between devices  22 us (22%)
  local copies, waits for them, and re-layouts  6.84 us (7%)
  other arithmetic  6.05 us (6%)
  matrix products  5.05 us (5%)
  starting transfers between devices  3.64 us (4%)
    all_to_all x1, blocking collectives, local(): lax.all_to_all(voltages, ('chan', 'bl'), split_axis=2, concat_axis=1, til...  56.5 us
    ppermute x1, waiting for transfers between devices, passed_along(): return lax.ppermute(block, axis, route)  22 us
    another operation x5, other arithmetic, local(): return jnp.stack([jnp.stack(real_list, 1), jnp.stack(imag_list, 1)], 0)  5.19 us
    dot_general x4, matrix products, products(): jnp.einsum('pct,qct->cpq', stacked, stacked, preferred_element_type=jnp.f...  5.05 us
    ppermute x1, starting transfers between devices, passed_along(): return lax.ppermute(block, axis, route)  3.64 us
    unnamed x1, local copies, waits for them, and re-layouts  2.76 us
    another operation x1, local copies, waits for them, and re-layouts, local(): return jnp.stack([jnp.stack(real_list, 1), jnp.stack(imag_list, 1)], 0)  2.29 us
  transfers between devices with their start and end apart: 1, of which 1 were waited for; matrix products, arithmetic and copies ran while one was open for 0% of the time, Pallas kernels for 0%

commit v1 on v0

v1 whole, which is shorter than its diff:
```python
import functools

import jax
import jax.numpy as jnp
from jax import lax
from jax.experimental import pallas as pl
from jax.experimental.pallas import tpu as pltpu
from jax.sharding import PartitionSpec as P

HALF = 128
ROWS = 16
MESH = pl.DeviceIdType.MESH


def tapers(length):
    steps = jnp.arange(length, dtype=jnp.float32)
    taper_early = jnp.sin(jnp.pi * (steps + 0.5) / (2.0 * length))
    taper_late = jnp.sin(jnp.pi * (steps + 0.5 + length) / (2.0 * length))
    return (taper_early, taper_late)


def flipped(index, mask, size):
    if size & (size - 1):
        return lax.rem(index + mask, size)
    total, bit = 0, 1
    while bit < size:
        total = total + ((index // bit + mask // bit) % 2) * bit
        bit *= 2
    return total


def exchange(n_tm, n_chan, n_bl, x_ref, taper_ref, y_ref, recv, halo, send_sem, recv_sem, halo_send, halo_recv):
    n = n_chan * n_bl
    tm, chan, bl = lax.axis_index("tm"), lax.axis_index("chan"), lax.axis_index("bl")
    rank = chan * n_bl + bl
    own = x_ref.shape[1]
    chans = x_ref.shape[2] // n
    halves = x_ref.shape[3] // HALF
    group = ROWS // own
    n_groups = n // group

    def peer(step):
        there = flipped(bl, step // n_chan, n_bl)
        return flipped(chan, step % n_chan, n_chan), there

    barrier = pltpu.get_barrier_semaphore()

    def greet(step, carry):
        c, b = peer(step)
        pl.semaphore_signal(barrier, inc=1, device_id={"chan": c, "bl": b}, device_id_type=MESH)
        return carry

    lax.fori_loop(1, n, greet, 0)

    @pl.when(tm + 1 < n_tm)
    def _():
        pl.semaphore_signal(barrier, inc=1, device_id={"tm": tm + 1}, device_id_type=MESH)

    @pl.when(tm > 0)
    def _():
        pl.semaphore_signal(barrier, inc=1, device_id={"tm": tm - 1}, device_id_type=MESH)

    pl.semaphore_wait(barrier, n - 1 + jnp.minimum(tm, 1) + jnp.minimum(n_tm - 1 - tm, 1))

    def block(half, target):
        return x_ref.at[:, :, pl.ds(pl.multiple_of(target * chans, chans), chans), pl.ds(half * HALF, HALF)]

    def slot(half, source):
        return recv.at[half, :, pl.ds(source * own, own)]

    def outgoing(half, step):
        c, b = peer(step)
        return pltpu.make_async_remote_copy(
            src_ref=block(half, c * n_bl + b),
            dst_ref=slot(half, rank),
            send_sem=send_sem.at[half, step],
            recv_sem=recv_sem.at[half, rank],
            device_id={"chan": c, "bl": b},
            device_id_type=MESH,
        )

    for half in reversed(range(halves)):
        pltpu.make_async_copy(block(half, rank), slot(half, rank), recv_sem.at[half, rank]).start()

        def launch(step, carry):
            outgoing(half, step).start()
            return carry

        lax.fori_loop(1, n, launch, 0)

    def group_at(step):
        if group == 1:
            c, b = peer(step)
            return c * n_bl + b
        return lax.rem(rank // group + step, n_groups)

    def arrive(half, which):
        for member in range(group):
            source = which * group + member
            pltpu.make_async_copy(block(half, rank), slot(half, source), recv_sem.at[half, source]).wait()

    def rows(which):
        return pl.ds(pl.multiple_of(which * ROWS, ROWS), ROWS)

    def forward(which):
        return pltpu.make_async_remote_copy(
            src_ref=recv.at[halves - 1, :, rows(which)],
            dst_ref=halo.at[:, rows(which)],
            send_sem=halo_send.at[which],
            recv_sem=halo_recv.at[which],
            device_id={"tm": tm + 1},
            device_id_type=MESH,
        )

    def put(values, which, window, column, taper):
        for part in range(2):
            turned = jnp.swapaxes(values[part] * taper, 0, 1).astype(jnp.bfloat16)
            y_ref[window, :, rows(which), column + part * HALF : column + (part + 1) * HALF] = turned

    early = taper_ref[0:1, :].reshape(1, 1, HALF)
    late = taper_ref[1:2, :].reshape(1, 1, HALF)

    def last_half(step, carry):
        which = group_at(step)
        arrive(halves - 1, which)

        @pl.when(tm + 1 < n_tm)
        def _():
            forward(which).start()

        values = recv[halves - 1, :, rows(which)].astype(jnp.float32)
        put(values, which, halves - 1, 0, late)
        return carry

    lax.fori_loop(0, n_groups, last_half, 0)

    for half in range(halves - 1):

        def other_half(step, carry):
            which = group_at(step)
            arrive(half, which)
            values = recv[half, :, rows(which)].astype(jnp.float32)
            put(values, which, half, 0, late)
            put(values, which, half + 1, 2 * HALF, early)
            if half == 0:

                @pl.when(tm > 0)
                def _():
                    forward(which).wait_recv()
                    put(halo[:, rows(which)].astype(jnp.float32), which, 0, 2 * HALF, early)

                @pl.when(tm == 0)
                def _():
                    y_ref[0, :, rows(which), 2 * HALF :] = jnp.zeros((chans, ROWS, 2 * HALF), jnp.bfloat16)

            return carry

        lax.fori_loop(0, n_groups, other_half, 0)

    for half in range(halves):

        def sent(step, carry):
            outgoing(half, step).wait_send()
            return carry

        lax.fori_loop(1, n, sent, 0)

    @pl.when(tm + 1 < n_tm)
    def _():
        def passed(step, carry):
            forward(step).wait_send()
            return carry

        lax.fori_loop(0, n_groups, passed, 0)


def correlate(y_ref, out_ref):
    scale = 1.0 / HALF
    for window in range(y_ref.shape[0]):
        y = y_ref[window, 0]
        a_late, b_late = y[:, :HALF], y[:, HALF : 2 * HALF]
        a_early, b_early = y[:, 2 * HALF : 3 * HALF], y[:, 3 * HALF :]
        swapped = jnp.concatenate([b_late, -a_late, b_early, -a_early], axis=1)
        dims = (((1,), (1,)), ((), ()))
        real = lax.dot_general(y, y, dims, preferred_element_type=jnp.float32)
        imag = lax.dot_general(swapped, y, dims, preferred_element_type=jnp.float32)
        out_ref[0, 0, window] = (real * scale).astype(out_ref.dtype)
        out_ref[1, 0, window] = (imag * scale).astype(out_ref.dtype)


def solution(mesh):
    n_tm, n_chan, n_bl = (mesh.shape[axis] for axis in ("tm", "chan", "bl"))
    n = n_chan * n_bl

    def local(voltages):
        own, channels, samples = voltages.shape[1:]
        signals = own * n
        chans = channels // n
        halves = samples // HALF
        n_groups = signals // ROWS
        block = (signals, chans, HALF)
        y = pl.pallas_call(
            functools.partial(exchange, n_tm, n_chan, n_bl),
            out_shape=jax.ShapeDtypeStruct((halves, chans, signals, 4 * HALF), jnp.bfloat16),
            in_specs=[pl.BlockSpec(memory_space=pl.ANY), pl.BlockSpec(memory_space=pltpu.VMEM)],
            out_specs=pl.BlockSpec(memory_space=pltpu.VMEM),
            scratch_shapes=[
                pltpu.VMEM((halves, 2) + block, jnp.bfloat16),
                pltpu.VMEM((2,) + block, jnp.bfloat16),
                pltpu.SemaphoreType.DMA((halves, n)),
                pltpu.SemaphoreType.DMA((halves, n)),
                pltpu.SemaphoreType.DMA((n_groups,)),
                pltpu.SemaphoreType.DMA((n_groups,)),
            ],
            compiler_params=pltpu.CompilerParams(
                collective_id=0, has_side_effects=True, vmem_limit_bytes=32 * 1024 * 1024
            ),
        )(voltages, jnp.stack(tapers(HALF)))
        return pl.pallas_call(
            correlate,
            grid=(chans,),
            out_shape=jax.ShapeDtypeStruct((2, chans, halves, signals, signals), jnp.bfloat16),
            in_specs=[pl.BlockSpec((halves, 1, signals, 4 * HALF), lambda c: (0, c, 0, 0))],
            out_specs=pl.BlockSpec((2, 1, halves, signals, signals), lambda c: (0, c, 0, 0, 0)),
            compiler_params=pltpu.CompilerParams(vmem_limit_bytes=32 * 1024 * 1024),
        )(y)

    return jax.shard_map(
        local,
        mesh=mesh,
        in_specs=(P(None, ("chan", "bl"), None, "tm"),),
        out_specs=P(None, ("chan", "bl"), "tm", None, None),
        check_vma=False,
    )
```

time: 100 us -> 60.1 us (0.60)
  the two profiles are of different devices: /device:TPU:0 before, /device:TPU:23 now
where the time goes in v1:
time: 60.1 us; the launch traced here: 59.9 us
  Pallas kernels  58.2 us (97%)
  local copies, waits for them, and re-layouts  1.59 us (3%)
    pallas_call x1, Pallas kernels, local(): pl.pallas_call(functools.partial(exchange, n_tm, n_chan, n_bl), out_shape...  52.5 us
    pallas_call x1, Pallas kernels, local(): pl.pallas_call(correlate, grid=(chans,), out_shape=jax.ShapeDtypeStruct((...  5.78 us
    unnamed x2, local copies, waits for them, and re-layouts  1.59 us

profile of v1, /device:TPU:23, one launch (start us, length us, event | category | flops | bytes accessed | tf_op | source)
XLA Modules:
  0.0 59.9 jit_solution(12506659497754592991)
XLA Ops:
  0.0 0.1 multiply_sine_fusion
  0.1 0.0 copy-start
  0.1 1.6 %copy-done = bf16[2,16,128,256]{3,2,1,0:T(8,128)(2,1)S(1)} copy-done((bf16[2,16,128,256]{3,2,1,0:T(8,128)(2,1)S(1)}, bf16[2,16,128,256]{3,2,1,0:T(8,128)(2,1)}, u32[]{:S(2)}) %copy-start) | copy-done | bytes 2097176
  1.7 52.5 %shard_map.17.y_ref = bf16[2,8,256,512]{3,2,1,0:T(8,128)(2,1)S(1)} custom-call(bf16[2,16,128,256]{3,2,1,0:T(8,128)(2,1)S(1)} %copy-done, f32[2,128]{1,0:T(2,128)S(1)} %pad_maximum_fusion.taper_ref), custom_call_target="tpu_custom_call" | custom-call | tf_op jit(solution)/shard_map/pallas_call | solution.py:202
  54.1 5.8 %shard_map.18 = bf16[2,8,2,256,256]{4,3,2,1,0:T(8,128)(2,1)} custom-call(bf16[2,8,256,512]{3,2,1,0:T(8,128)(2,1)S(1)} %shard_map.17.y_ref), custom_call_target="tpu_custom_call" | custom-call | tf_op jit(solution)/shard_map/pallas_call | solution.py:219
  (1 shorter events, 0.0 us)
Async XLA Ops:
  0.1 1.6 %copy-start = (bf16[2,16,128,256]{3,2,1,0:T(8,128)(2,1)S(1)}, bf16[2,16,128,256]{3,2,1,0:T(8,128)(2,1)}, u32[]{:S(2)}) copy-start(bf16[2,16,128,256]{3,2,1,0:T(8,128)(2,1)} %x_ref.1) | copy-start | bytes 6291460

commit v2 on v1

--- a/solution.py
+++ b/solution.py
@@ -9,6 +9,7 @@
 
 HALF = 128
 ROWS = 16
+MIB = 1024 * 1024
 MESH = pl.DeviceIdType.MESH
 
 
@@ -29,7 +30,7 @@
     return total
 
 
-def exchange(n_tm, n_chan, n_bl, x_ref, taper_ref, y_ref, recv, halo, send_sem, recv_sem, halo_send, halo_recv):
+def exchange(n_tm, n_chan, n_bl, source_ref, taper_ref, y_ref, x_ref, recv, halo, load_sem, send_sem, recv_sem, halo_send, halo_recv):
     n = n_chan * n_bl
     tm, chan, bl = lax.axis_index("tm"), lax.axis_index("chan"), lax.axis_index("bl")
     rank = chan * n_bl + bl
@@ -43,6 +44,8 @@
         there = flipped(bl, step // n_chan, n_bl)
         return flipped(chan, step % n_chan, n_chan), there
 
+    load = pltpu.make_async_copy(source_ref, x_ref, load_sem)
+    load.start()
     barrier = pltpu.get_barrier_semaphore()
 
     def greet(step, carry):
@@ -61,6 +64,7 @@
         pl.semaphore_signal(barrier, inc=1, device_id={"tm": tm - 1}, device_id_type=MESH)
 
     pl.semaphore_wait(barrier, n - 1 + jnp.minimum(tm, 1) + jnp.minimum(n_tm - 1 - tm, 1))
+    load.wait()
 
     def block(half, target):
         return x_ref.at[:, :, pl.ds(pl.multiple_of(target * chans, chans), chans), pl.ds(half * HALF, HALF)]
@@ -176,16 +180,18 @@
 
 def correlate(y_ref, out_ref):
     scale = 1.0 / HALF
+    signals = y_ref.shape[2]
+    c = pl.program_id(0)
     for window in range(y_ref.shape[0]):
-        y = y_ref[window, 0]
+        y = y_ref[window, c]
         a_late, b_late = y[:, :HALF], y[:, HALF : 2 * HALF]
         a_early, b_early = y[:, 2 * HALF : 3 * HALF], y[:, 3 * HALF :]
         swapped = jnp.concatenate([b_late, -a_late, b_early, -a_early], axis=1)
+        both = jnp.concatenate([y, swapped], axis=0)
         dims = (((1,), (1,)), ((), ()))
-        real = lax.dot_general(y, y, dims, preferred_element_type=jnp.float32)
-        imag = lax.dot_general(swapped, y, dims, preferred_element_type=jnp.float32)
-        out_ref[0, 0, window] = (real * scale).astype(out_ref.dtype)
-        out_ref[1, 0, window] = (imag * scale).astype(out_ref.dtype)
+        gram = lax.dot_general(both, y, dims, preferred_element_type=jnp.float32) * scale
+        out_ref[0, 0, window] = gram[:signals].astype(out_ref.dtype)
+        out_ref[1, 0, window] = gram[signals:].astype(out_ref.dtype)
 
 
 def solution(mesh):
@@ -202,27 +208,29 @@
         y = pl.pallas_call(
             functools.partial(exchange, n_tm, n_chan, n_bl),
             out_shape=jax.ShapeDtypeStruct((halves, chans, signals, 4 * HALF), jnp.bfloat16),
-            in_specs=[pl.BlockSpec(memory_space=pl.ANY), pl.BlockSpec(memory_space=pltpu.VMEM)],
+            in_specs=[pl.BlockSpec(memory_space=pltpu.HBM), pl.BlockSpec(memory_space=pltpu.VMEM)],
             out_specs=pl.BlockSpec(memory_space=pltpu.VMEM),
             scratch_shapes=[
+                pltpu.VMEM(voltages.shape, jnp.bfloat16),
                 pltpu.VMEM((halves, 2) + block, jnp.bfloat16),
                 pltpu.VMEM((2,) + block, jnp.bfloat16),
+                pltpu.SemaphoreType.DMA,
                 pltpu.SemaphoreType.DMA((halves, n)),
                 pltpu.SemaphoreType.DMA((halves, n)),
                 pltpu.SemaphoreType.DMA((n_groups,)),
                 pltpu.SemaphoreType.DMA((n_groups,)),
             ],
             compiler_params=pltpu.CompilerParams(
-                collective_id=0, has_side_effects=True, vmem_limit_bytes=32 * 1024 * 1024
+                collective_id=0, has_side_effects=True, vmem_limit_bytes=32 * MIB
             ),
-        )(voltages, jnp.stack(tapers(HALF)))
+        )(pltpu.with_memory_space_constraint(voltages, pltpu.HBM), jnp.stack(tapers(HALF)))
         return pl.pallas_call(
             correlate,
             grid=(chans,),
             out_shape=jax.ShapeDtypeStruct((2, chans, halves, signals, signals), jnp.bfloat16),
-            in_specs=[pl.BlockSpec((halves, 1, signals, 4 * HALF), lambda c: (0, c, 0, 0))],
+            in_specs=[pl.BlockSpec(memory_space=pltpu.VMEM)],
             out_specs=pl.BlockSpec((2, 1, halves, signals, signals), lambda c: (0, c, 0, 0, 0)),
-            compiler_params=pltpu.CompilerParams(vmem_limit_bytes=32 * 1024 * 1024),
+            compiler_params=pltpu.CompilerParams(vmem_limit_bytes=32 * MIB),
         )(y)
 
     return jax.shard_map(

time: 60.1 us -> 59 us (0.982)
  local copies, waits for them, and re-layouts: 1.59 us -> 0 us
    unnamed x2 -> x0, local copies, waits for them, and re-layouts: 1.59 us -> none
    pallas_call x1, Pallas kernels: 52.5 us -> 53.2 us  [local(): pl.pallas_call(functools.partial(exchange, n_tm, n_chan, n_bl), out_shape...]
where the time goes in v2:
time: 59 us; the launch traced here: 58.8 us
  Pallas kernels  58.8 us (100%)
    pallas_call x1, Pallas kernels, local(): pl.pallas_call(functools.partial(exchange, n_tm, n_chan, n_bl), out_shape...  53.2 us
    pallas_call x1, Pallas kernels, local(): pl.pallas_call(correlate, grid=(chans,), out_shape=jax.ShapeDtypeStruct((...  5.61 us

profile of v2, /device:TPU:23, one launch (start us, length us, event | category | flops | bytes accessed | tf_op | source)
XLA Modules:
  0.0 58.8 jit_solution(920405132525641915)
XLA Ops:
  0.0 0.1 multiply_sine_fusion
  0.1 53.2 %shard_map.17.y_ref = bf16[2,8,256,512]{3,2,1,0:T(8,128)(2,1)S(1)} custom-call(bf16[2,16,128,256]{3,2,1,0:T(8,128)(2,1)} %source_ref.1, f32[2,128]{1,0:T(2,128)S(1)} %pad_maximum_fusion.taper_ref), custom_call_target="tpu_custom_call" | custom-call | tf_op jit(solution)/shard_map/pallas_call | solution.py:208
  53.2 5.6 %shard_map.18 = bf16[2,8,2,256,256]{4,3,2,1,0:T(8,128)(2,1)} custom-call(bf16[2,8,256,512]{3,2,1,0:T(8,128)(2,1)S(1)} %shard_map.17.y_ref), custom_call_target="tpu_custom_call" | custom-call | tf_op jit(solution)/shard_map/pallas_call | solution.py:227
  (1 shorter events, 0.0 us)

commit v3 on v2

--- a/solution.py
+++ b/solution.py
@@ -30,7 +30,13 @@
     return total
 
 
-def exchange(n_tm, n_chan, n_bl, source_ref, taper_ref, y_ref, x_ref, recv, halo, load_sem, send_sem, recv_sem, halo_send, halo_recv):
+def gram(y):
+    swapped = jnp.concatenate([y[:, HALF:], -y[:, :HALF]], axis=1)
+    dims = (((1,), (1,)), ((), ()))
+    return lax.dot_general(jnp.concatenate([y, swapped], axis=0), y, dims, preferred_element_type=jnp.float32)
+
+
+def exchange(n_tm, n_chan, n_bl, source_ref, taper_ref, y_ref, part_ref, x_ref, aside, recv, halo, load_sem, send_sem, recv_sem, halo_send, halo_recv):
     n = n_chan * n_bl
     tm, chan, bl = lax.axis_index("tm"), lax.axis_index("chan"), lax.axis_index("bl")
     rank = chan * n_bl + bl
@@ -83,14 +89,17 @@
             device_id_type=MESH,
         )
 
-    for half in reversed(range(halves)):
+    for half in range(halves):
         pltpu.make_async_copy(block(half, rank), slot(half, rank), recv_sem.at[half, rank]).start()
 
-        def launch(step, carry):
-            outgoing(half, step).start()
-            return carry
-
-        lax.fori_loop(1, n, launch, 0)
+    for first, last in ((1, n // 2), (n // 2, n)):
+        for half in reversed(range(halves)):
+
+            def launch(step, carry):
+                outgoing(half, step).start()
+                return carry
+
+            lax.fori_loop(first, last, launch, 0)
 
     def group_at(step):
         if group == 1:
@@ -116,50 +125,63 @@
             device_id_type=MESH,
         )
 
-    def put(values, which, window, column, taper):
+    def turn(values):
+        return [jnp.swapaxes(values[part].astype(jnp.float32), 0, 1) for part in range(2)]
+
+    def put(turned, where, which, column, taper):
         for part in range(2):
-            turned = jnp.swapaxes(values[part] * taper, 0, 1).astype(jnp.bfloat16)
-            y_ref[window, :, rows(which), column + part * HALF : column + (part + 1) * HALF] = turned
+            tapered = (turned[part] * taper).astype(jnp.bfloat16)
+            where[:, rows(which), column + part * HALF : column + (part + 1) * HALF] = tapered
 
     early = taper_ref[0:1, :].reshape(1, 1, HALF)
     late = taper_ref[1:2, :].reshape(1, 1, HALF)
 
     def last_half(step, carry):
         which = group_at(step)
-        arrive(halves - 1, which)
+        arrive(1, which)
 
         @pl.when(tm + 1 < n_tm)
         def _():
             forward(which).start()
 
-        values = recv[halves - 1, :, rows(which)].astype(jnp.float32)
-        put(values, which, halves - 1, 0, late)
+        put(turn(recv[1, :, rows(which)]), aside, which, 0, late)
         return carry
 
     lax.fori_loop(0, n_groups, last_half, 0)
 
-    for half in range(halves - 1):
-
-        def other_half(step, carry):
+    def partial(window):
+        def one(c, carry):
+            part_ref[window, c] = gram(aside[c])
+            return carry
+
+        lax.fori_loop(0, chans, one, 0)
+
+    partial(1)
+
+    @pl.when(tm > 0)
+    def _():
+        def before(step, carry):
             which = group_at(step)
-            arrive(half, which)
-            values = recv[half, :, rows(which)].astype(jnp.float32)
-            put(values, which, half, 0, late)
-            put(values, which, half + 1, 2 * HALF, early)
-            if half == 0:
-
-                @pl.when(tm > 0)
-                def _():
-                    forward(which).wait_recv()
-                    put(halo[:, rows(which)].astype(jnp.float32), which, 0, 2 * HALF, early)
-
-                @pl.when(tm == 0)
-                def _():
-                    y_ref[0, :, rows(which), 2 * HALF :] = jnp.zeros((chans, ROWS, 2 * HALF), jnp.bfloat16)
-
-            return carry
-
-        lax.fori_loop(0, n_groups, other_half, 0)
+            forward(which).wait_recv()
+            put(turn(halo[:, rows(which)]), aside, which, 0, early)
+            return carry
+
+        lax.fori_loop(0, n_groups, before, 0)
+        partial(0)
+
+    @pl.when(tm == 0)
+    def _():
+        part_ref[0] = jnp.zeros(part_ref.shape[1:], jnp.float32)
+
+    def first_half(step, carry):
+        which = group_at(step)
+        arrive(0, which)
+        turned = turn(recv[0, :, rows(which)])
+        put(turned, y_ref, which, 0, late)
+        put(turned, y_ref, which, 2 * HALF, early)
+        return carry
+
+    lax.fori_loop(0, n_groups, first_half, 0)
 
     for half in range(halves):
 
@@ -178,20 +200,15 @@
         lax.fori_loop(0, n_groups, passed, 0)
 
 
-def correlate(y_ref, out_ref):
+def correlate(y_ref, part_ref, out_ref):
     scale = 1.0 / HALF
-    signals = y_ref.shape[2]
+    signals = y_ref.shape[1]
     c = pl.program_id(0)
-    for window in range(y_ref.shape[0]):
-        y = y_ref[window, c]
-        a_late, b_late = y[:, :HALF], y[:, HALF : 2 * HALF]
-        a_early, b_early = y[:, 2 * HALF : 3 * HALF], y[:, 3 * HALF :]
-        swapped = jnp.concatenate([b_late, -a_late, b_early, -a_early], axis=1)
-        both = jnp.concatenate([y, swapped], axis=0)
-        dims = (((1,), (1,)), ((), ()))
-        gram = lax.dot_general(both, y, dims, preferred_element_type=jnp.float32) * scale
-        out_ref[0, 0, window] = gram[:signals].astype(out_ref.dtype)
-        out_ref[1, 0, window] = gram[signals:].astype(out_ref.dtype)
+    for window in range(2):
+        both = gram(y_ref[c, :, 2 * window * HALF : 2 * (window + 1) * HALF])
+        total = (both + part_ref[window, c]) * scale
+        out_ref[0, 0, window] = total[:signals].astype(out_ref.dtype)
+        out_ref[1, 0, window] = total[signals:].astype(out_ref.dtype)
 
 
 def solution(mesh):
@@ -205,13 +222,18 @@
         halves = samples // HALF
         n_groups = signals // ROWS
         block = (signals, chans, HALF)
-        y = pl.pallas_call(
+        assert halves == 2
+        y, partial = pl.pallas_call(
             functools.partial(exchange, n_tm, n_chan, n_bl),
-            out_shape=jax.ShapeDtypeStruct((halves, chans, signals, 4 * HALF), jnp.bfloat16),
+            out_shape=(
+                jax.ShapeDtypeStruct((chans, signals, 4 * HALF), jnp.bfloat16),
+                jax.ShapeDtypeStruct((2, chans, 2 * signals, signals), jnp.float32),
+            ),
             in_specs=[pl.BlockSpec(memory_space=pltpu.HBM), pl.BlockSpec(memory_space=pltpu.VMEM)],
-            out_specs=pl.BlockSpec(memory_space=pltpu.VMEM),
+            out_specs=(pl.BlockSpec(memory_space=pltpu.VMEM), pl.BlockSpec(memory_space=pltpu.VMEM)),
             scratch_shapes=[
                 pltpu.VMEM(voltages.shape, jnp.bfloat16),
+                pltpu.VMEM((chans, signals, 2 * HALF), jnp.bfloat16),
                 pltpu.VMEM((halves, 2) + block, jnp.bfloat16),
                 pltpu.VMEM((2,) + block, jnp.bfloat16),
                 pltpu.SemaphoreType.DMA,
@@ -221,17 +243,17 @@
                 pltpu.SemaphoreType.DMA((n_groups,)),
             ],
             compiler_params=pltpu.CompilerParams(
-                collective_id=0, has_side_effects=True, vmem_limit_bytes=32 * MIB
+                collective_id=0, has_side_effects=True, vmem_limit_bytes=24 * MIB
             ),
         )(pltpu.with_memory_space_constraint(voltages, pltpu.HBM), jnp.stack(tapers(HALF)))
         return pl.pallas_call(
             correlate,
             grid=(chans,),
             out_shape=jax.ShapeDtypeStruct((2, chans, halves, signals, signals), jnp.bfloat16),
-            in_specs=[pl.BlockSpec(memory_space=pltpu.VMEM)],
+            in_specs=[pl.BlockSpec(memory_space=pltpu.VMEM), pl.BlockSpec(memory_space=pltpu.VMEM)],
             out_specs=pl.BlockSpec((2, 1, halves, signals, signals), lambda c: (0, c, 0, 0, 0)),
-            compiler_params=pltpu.CompilerParams(vmem_limit_bytes=32 * MIB),
-        )(y)
+            compiler_params=pltpu.CompilerParams(vmem_limit_bytes=24 * MIB),
+        )(y, partial)
 
     return jax.shard_map(
         local,

time: 59 us -> 58.4 us (0.990)
  Pallas kernels: 58.8 us -> 58.2 us
    pallas_call x1, Pallas kernels: 5.61 us -> 4.88 us  [local(): pl.pallas_call(correlate, grid=(chans,), out_shape=jax.ShapeDtypeStruct((...]
where the time goes in v3:
time: 58.4 us; the launch traced here: 58.3 us
  Pallas kernels  58.2 us (100%)
    pallas_call x1, Pallas kernels, local(): pl.pallas_call(functools.partial(exchange, n_tm, n_chan, n_bl), out_shape...  53.3 us
    pallas_call x1, Pallas kernels, local(): pl.pallas_call(correlate, grid=(chans,), out_shape=jax.ShapeDtypeStruct((...  4.88 us

profile of v3, /device:TPU:23, one launch (start us, length us, event | category | flops | bytes accessed | tf_op | source)
XLA Modules:
  0.0 58.3 jit_solution(13342631938636580963)
XLA Ops:
  0.0 0.1 multiply_sine_fusion
  0.1 53.3 %shard_map.17 = (bf16[8,256,512]{2,1,0:T(8,128)(2,1)S(1)}, f32[2,8,512,256]{3,2,1,0:T(8,128)S(1)}) custom-call(bf16[2,16,128,256]{3,2,1,0:T(8,128)(2,1)} %source_ref.1, f32[2,128]{1,0:T(2,128)S(1)} %pad_maximum_fusion.taper_ref), custom_call_target="tpu_custom_call" | custom-call | tf_op jit(solution)/shard_map/pallas_call | solution.py:226
  53.4 4.9 %shard_map.18 = bf16[2,8,2,256,256]{4,3,2,1,0:T(8,128)(2,1)} custom-call(bf16[8,256,512]{2,1,0:T(8,128)(2,1)S(1)} %get-tuple-element.7.y_ref, f32[2,8,512,256]{3,2,1,0:T(8,128)S(1)} %get-tuple-element.8.part_ref), custom_call_target="tpu_custom_call" | custom-call | tf_op jit(solution)/shard_map/pallas_call | solution.py:249
  (1 shorter events, 0.0 us)

commit v4 on v3

--- a/solution.py
+++ b/solution.py
@@ -92,14 +92,20 @@
     for half in range(halves):
         pltpu.make_async_copy(block(half, rank), slot(half, rank), recv_sem.at[half, rank]).start()
 
-    for first, last in ((1, n // 2), (n // 2, n)):
+    inner = jnp.minimum(jnp.minimum(bl, n_bl - 1 - bl), 1)
+    for offset in (inner, 1 - inner):
         for half in reversed(range(halves)):
 
-            def launch(step, carry):
-                outgoing(half, step).start()
+            def launch(index, carry):
+                step = index + offset * (n // 2)
+
+                @pl.when(step > 0)
+                def _():
+                    outgoing(half, step).start()
+
                 return carry
 
-            lax.fori_loop(first, last, launch, 0)
+            lax.fori_loop(0, n // 2, launch, 0)
 
     def group_at(step):
         if group == 1:

time: 58.4 us -> 58 us (level)
  no operation moved by 1% of the time
where the time goes in v4:
time: 58 us; the launch traced here: 57.9 us
  Pallas kernels  57.8 us (100%)
    pallas_call x1, Pallas kernels, local(): pl.pallas_call(functools.partial(exchange, n_tm, n_chan, n_bl), out_shape...  52.9 us
    pallas_call x1, Pallas kernels, local(): pl.pallas_call(correlate, grid=(chans,), out_shape=jax.ShapeDtypeStruct((...  4.88 us

profile of v4, /device:TPU:23, one launch (start us, length us, event | category | flops | bytes accessed | tf_op | source)
XLA Modules:
  0.0 57.9 jit_solution(4926071229661844575)
XLA Ops:
  0.0 0.1 multiply_sine_fusion
  0.1 52.9 %shard_map.17 = (bf16[8,256,512]{2,1,0:T(8,128)(2,1)S(1)}, f32[2,8,512,256]{3,2,1,0:T(8,128)S(1)}) custom-call(bf16[2,16,128,256]{3,2,1,0:T(8,128)(2,1)} %source_ref.1, f32[2,128]{1,0:T(2,128)S(1)} %pad_maximum_fusion.taper_ref), custom_call_target="tpu_custom_call" | custom-call | tf_op jit(solution)/shard_map/pallas_call | solution.py:232
  53.0 4.9 %shard_map.18 = bf16[2,8,2,256,256]{4,3,2,1,0:T(8,128)(2,1)} custom-call(bf16[8,256,512]{2,1,0:T(8,128)(2,1)S(1)} %get-tuple-element.7.y_ref, f32[2,8,512,256]{3,2,1,0:T(8,128)S(1)} %get-tuple-element.8.part_ref), custom_call_target="tpu_custom_call" | custom-call | tf_op jit(solution)/shard_map/pallas_call | solution.py:255
  (1 shorter events, 0.0 us)
